TPU v7x, 128 devices: a whole 4x4x4 slice. The times are simulated.
128 devices in a mesh: seq: 16 (over y, z_lo, core), tensor: 8 (over z_hi, x).
Axes of the slice: x: 4, y: 4, z: 4 (z_hi: 2, z_lo: 2; z = z_hi * 2 + z_lo), core: 2. Of those that a mesh axis runs over, the one named last changes fastest.
Arguments:
- tokens: bfloat16 [8192, 8192], P('seq', 'tensor'), may hold values from -6 to 6
- positions: int32 [8192], P('seq'), may hold values from 0 to 8191, each once
- norm_gain: float32 [8192], replicated, may hold values from 0.1 to 1.9
- w_query: bfloat16 [8192, 4096], P('seq', 'tensor'), may hold values from -0.0625 to 0.0625
- w_key: bfloat16 [8192, 1024], P('seq', 'tensor'), may hold values from -0.0625 to 0.0625
- w_value: bfloat16 [8192, 1024], P('seq', 'tensor'), may hold values from -0.0625 to 0.0625
- b_query: float32 [4096], P('tensor'), may hold values from -40 to 40
- b_key: float32 [1024], P('tensor'), may hold values from -40 to 40
- b_value: float32 [1024], P('tensor'), may hold values from -6 to 6
- w_out: bfloat16 [4096, 8192], P('tensor', 'seq'), may hold values from -0.09375 to 0.09375
Outputs:
- mixed: bfloat16 [8192, 8192], P('seq', 'tensor')
- context: bfloat16 [8192, 4096], P('seq', 'tensor')
Inputs may be any that keep to these rules, and one draw needn't show every extreme that they name: positions holds every position 0 to 8191 once.
All inputs are finite; a program needn't handle non-finite values.
Results may differ from a plain program's by a relative error of at most 0.025.
Values may be sent and summed in bfloat16 or wider, within the bound.
No kernel may reach another device: no remote copies, remote signals or barrier semaphores. Data moves between devices by JAX's collectives and lax.ppermute only.
A program may use at most 128 MiB of HBM per device.

v0:
```python
import math
import jax
import jax.numpy as jnp
from jax import lax
from jax.sharding import PartitionSpec as P

HD = 128
NORM_EPS = 1e-06
ROPE_BASE = 1000000.0
NEG_FILL = -1e30


def sent_together(arrays, axis, dim, along):
    ends, at = ([], 0)
    for a in arrays[:-1]:
        at += a.shape[along]
        ends.append(at)
    both = jnp.concatenate(arrays, axis=along)
    return tuple(jnp.split(lax.all_gather(both, axis, axis=dim, tiled=True), ends, axis=along))


def rotate(values_in, positions):
    half_dim = HD // 2
    inv_freq = ROPE_BASE ** (-jnp.arange(half_dim, dtype=jnp.float32) * 2.0 / HD)
    angles = positions.astype(jnp.float32)[:, None] * inv_freq[None, :]
    cosine = jnp.cos(angles)[:, None, :]
    sines = jnp.sin(angles)[:, None, :]
    lower_half = values_in[..., :half_dim]
    upper_half = values_in[..., half_dim:]
    return jnp.concatenate(
        [lower_half * cosine - upper_half * sines, upper_half * cosine + lower_half * sines], -1
    )


def shards(tokens, positions, norm_gain, w_query, w_key, w_value, b_query, b_key, b_value, w_out):
    tok_rows = tokens.shape[0]
    features = lax.all_gather(tokens, "tensor", axis=1, tiled=True)
    inputs = features.astype(jnp.float32)
    inverse_rms = lax.rsqrt(jnp.mean(inputs * inputs, -1, keepdims=True) + NORM_EPS)
    normed = (inputs * inverse_rms * norm_gain[None, :]).astype(jnp.bfloat16)
    w_cat = jnp.concatenate((w_query, w_key, w_value), 1)
    b_cat = jnp.concatenate((b_query, b_key, b_value))
    projected = jnp.dot(
        normed, lax.all_gather(w_cat, "seq", axis=0, tiled=True), preferred_element_type=jnp.float32
    )
    projected = projected + b_cat[None, :]
    query_cols = w_query.shape[1]
    key_cols = w_key.shape[1]
    heads_here = query_cols // HD
    kv_here = key_cols // HD
    group = heads_here // kv_here
    queries = rotate(projected[:, :query_cols].reshape(tok_rows, heads_here, HD), positions).astype(
        jnp.bfloat16
    )
    queries = queries.reshape(tok_rows, kv_here, group, HD)
    keys_rot = rotate(
        projected[:, query_cols : query_cols + key_cols].reshape(tok_rows, kv_here, HD), positions
    ).astype(jnp.bfloat16)
    values = (
        projected[:, query_cols + key_cols :].astype(jnp.bfloat16).reshape(tok_rows, kv_here, HD)
    )
    scale = HD ** (-0.5)

    def attend_block(running, key_block):
        running_max, denominator, numerator = running
        block_keys, block_values, key_pos = key_block
        scores = (
            jnp.einsum("tgcd,sgd->gcts", queries, block_keys, preferred_element_type=jnp.float32)
            * scale
        )
        allowed = (key_pos[None, :] <= positions[:, None])[None, None, :, :]
        scores = jnp.where(allowed, scores, NEG_FILL)
        new_max = jnp.maximum(running_max, jnp.max(scores, -1))
        weights = jnp.where(allowed, jnp.exp(scores - new_max[..., None]), 0.0)
        rescale = jnp.exp(running_max - new_max)
        denominator = denominator * rescale + jnp.sum(weights, -1)
        numerator = numerator * rescale[..., None] + jnp.einsum(
            "gcts,sgd->gctd",
            weights.astype(jnp.bfloat16),
            block_values,
            preferred_element_type=jnp.float32,
        )
        return (new_max, denominator, numerator)

    start_state = (
        jnp.full((kv_here, group, tok_rows), NEG_FILL, jnp.float32),
        jnp.zeros((kv_here, group, tok_rows), jnp.float32),
        jnp.zeros((kv_here, group, tok_rows, HD), jnp.float32),
    )
    all_keys_in, all_values_in, key_pos = (
        *sent_together((keys_rot, values), "seq", 0, 1),
        lax.all_gather(positions, "seq", axis=0, tiled=True),
    )
    count = all_keys_in.shape[0]
    width = math.gcd(count, 2048)
    stacked = (
        all_keys_in.reshape(count // width, width, kv_here, HD),
        all_values_in.reshape(count // width, width, kv_here, HD),
        key_pos.reshape(count // width, width),
    )

    def stepper(carried, key_block):
        return (attend_block(carried, key_block), None)

    result, unused = lax.scan(stepper, start_state, stacked)
    unused_max, denominator, numerator = result
    per_head = numerator / denominator[..., None]
    context = (
        jnp.transpose(per_head, (2, 0, 1, 3))
        .reshape(tok_rows, heads_here * HD)
        .astype(jnp.bfloat16)
    )
    out_terms = jnp.dot(
        context,
        lax.all_gather(w_out, "seq", axis=1, tiled=True),
        preferred_element_type=jnp.float32,
    )
    summed = lax.psum_scatter(
        out_terms.astype(jnp.bfloat16), "tensor", scatter_dimension=1, tiled=True
    ).astype(jnp.float32)
    mixed = (tokens.astype(jnp.float32) + summed).astype(jnp.bfloat16)
    return (mixed, context)


def solution(mesh):
    in_specs = (
        P("seq", "tensor"),
        P("seq"),
        P(),
        P("seq", "tensor"),
        P("seq", "tensor"),
        P("seq", "tensor"),
        P("tensor"),
        P("tensor"),
        P("tensor"),
        P("tensor", "seq"),
    )
    out_specs = (P("seq", "tensor"), P("seq", "tensor"))
    return jax.shard_map(shards, mesh=mesh, in_specs=in_specs, out_specs=out_specs, check_vma=False)
```

profile of v0, /device:TPU:0, one launch (start us, length us, event | category | flops | bytes accessed | tf_op | source)
XLA Modules:
  0.0 495.2 jit_solution(8700985036103313961)
XLA Ops:
  11.6 109.7 %all-gather.6.cloned.1.call-done = bf16[512,8192]{1,0:T(8,128)(2,1)} async-done(((bf16[512,1024]{1,0:T(8,128)(2,1)}), bf16[512,8192]{1,0:T(8,128)(2,1)}) %all-gather.6.cloned.1.call-update) | async-done | bytes 8388624 | tf_op jit(solution)/shard_map/all_gather | solution.py:37
  121.2 5.1 %fusion.25 = f32[512]{0:T(512)S(1)} fusion(bf16[512,8192]{1,0:T(8,128)(2,1)} %all-gather.6.cloned.1.call-done), kind=kLoop, calls=%fused_computation.31 | loop fusion | flops 12582400 | bytes 8390656 | tf_op jit(solution)/shard_map/reduce_sum | solution.py:39
  126.4 66.7 %all-gather.8.cloned.1.call-done = bf16[8192,768]{1,0:T(8,128)(2,1)} async-done(((bf16[512,768]{1,0:T(8,128)(2,1)}), bf16[8192,768]{1,0:T(8,128)(2,1)}) %all-gather.8.cloned.1.call-update) | async-done | bytes 12582928 | tf_op jit(solution)/shard_map/all_gather | solution.py:44
  193.1 12.5 %fusion.32 = f32[512,768]{0,1:T(8,128)S(1)} fusion(bf16[8192,768]{1,0:T(8,128)(2,1)} %all-gather.8.cloned.1.call-done, bf16[512,8192]{1,0:T(8,128)(2,1)} %all-gather.6.cloned.1.call-done, f32[8192]{0:T(1024)S(1)} %copy-done.5, f32[512]{0:T(512)S(1)} %add_rsqrt_fusion, f32[768]{0:T(1024)S(1)} %pad_maximum_fusion.3), kind=kOutput, calls=%fused_computation.39 | convolution fusion | flops 6459621376 | bytes 22582272 | tf_op jit(solution)/shard_map/dot_general | solution.py:43
  208.6 19.0 %all-gather = s32[16,1,512]{2,1,0:T(1,128)S(1)} all-gather(s32[1,1,512]{2,1,0:T(1,128)S(1)} %bitcast.114), channel_id=1, replica_groups=mesh['seq'=16,'tensor'=8] {'seq'}, dimensions={0}, use_global_device_ids=true | all-gather | bytes 34816 | tf_op jit(solution)/shard_map/all_gather | solution.py:92
  230.0 15.2 %all-gather.10.cloned.1.call-done = bf16[8192,2,128]{0,2,1:T(8,128)(2,1)} async-done(((bf16[512,2,128]{0,2,1:T(8,128)(2,1)}), bf16[8192,2,128]{0,2,1:T(8,128)(2,1)}) %all-gather.10.cloned.1.call-update) | async-done | bytes 4194320 | tf_op jit(solution)/shard_map/all_gather | solution.py:19
  245.2 3.9 fusion.47
  249.2 4.1 copy.33
  255.7 103.9 %while.15 = (s32[]{:T(128)}, f32[1,4,512]{2,1,0:T(4,128)S(1)}, f32[1,4,512]{2,1,0:T(4,128)S(1)}, f32[1,4,512,128]{3,2,1,0:T(8,128)S(1)}, s32[4,2048]{1,0:T(4,128...) while((s32[]{:T(128)}, f32[1,4,512]{2,1,0:T(4,128)S(1)}, ...), condition=%wide.region_4.5_spmd.clone, body=%wide.region_1.4_spmd.clone.sunk | while | flops 2203856896 | bytes 125463704 | solution.py:105
  256.5 10.1 %fusion.60 = (f32[4,512]{1,0:T(4,128)S(1)}, f32[2048,512,4]{1,0,2:T(8,128)}) fusion(pred[512,2048]{0,1:T(8,128)(4,1)S(1)} %broadcast_compare_fusion.2, bf16[512,1,4,128]{3,0,2,1:T(8,128)(2,1)} %get-tuple-element.233, bf16[4,2048,1,128]{3,1,2,0:T(8,128)(2,1)} %get-tuple-element.232, s32[]{:T(128)} %get-tuple-element.215), kind=kOutput, calls=%fused_computation.2.clone.1 | convolution fusion | flops 1086322688 | bytes 18883072 | tf_op jit(solution)/shard_map/while/body/eval_jaxpr/tgcd,sgd->gcts/dot_general | solution.py:68
  266.6 9.0 %fusion.63 = f32[1,4,512,128]{3,2,1,0:T(8,128)S(1)} fusion(f32[2048,512,4]{1,0,2:T(8,128)} %get-tuple-element.202, f32[4,512]{1,0:T(4,128)S(1)} %bitcast.105, pred[512,2048]{0,1:T(8,128)(4,1)S(1)} %broadcast_compare_fusion.2, f32[1,4,512,128]{3,2,1,0:T(8,128)S(1)} %get-tuple-element.218, bf16[4,2048,1,128]{3,1,2,0:T(8,128)(2,1)} %get-tuple-element.234, ...), kind=kOutput, calls=%fused_computation.10.clone.1 | convolution fusion | flops 1095499776 | bytes 20464128 | tf_op jit(solution)/shard_map/while/body/eval_jaxpr/gcts,sgd->gctd/dot_general | solution.py:77
  277.9 4.2 fusion.62
  282.9 10.2 %fusion.60 = (f32[4,512]{1,0:T(4,128)S(1)}, f32[2048,512,4]{1,0,2:T(8,128)}) fusion(pred[512,2048]{0,1:T(8,128)(4,1)S(1)} %broadcast_compare_fusion.2, bf16[512,1,4,128]{3,0,2,1:T(8,128)(2,1)} %get-tuple-element.233, bf16[4,2048,1,128]{3,1,2,0:T(8,128)(2,1)} %get-tuple-element.232, s32[]{:T(128)} %get-tuple-element.215), kind=kOutput, calls=%fused_computation.2.clone.1 | convolution fusion | flops 1086322688 | bytes 18883072 | tf_op jit(solution)/shard_map/while/body/eval_jaxpr/tgcd,sgd->gcts/dot_general | solution.py:68
  293.1 8.8 %fusion.63 = f32[1,4,512,128]{3,2,1,0:T(8,128)S(1)} fusion(f32[2048,512,4]{1,0,2:T(8,128)} %get-tuple-element.202, f32[4,512]{1,0:T(4,128)S(1)} %bitcast.105, pred[512,2048]{0,1:T(8,128)(4,1)S(1)} %broadcast_compare_fusion.2, f32[1,4,512,128]{3,2,1,0:T(8,128)S(1)} %get-tuple-element.218, bf16[4,2048,1,128]{3,1,2,0:T(8,128)(2,1)} %get-tuple-element.234, ...), kind=kOutput, calls=%fused_computation.10.clone.1 | convolution fusion | flops 1095499776 | bytes 20464128 | tf_op jit(solution)/shard_map/while/body/eval_jaxpr/gcts,sgd->gctd/dot_general | solution.py:77
  304.0 4.2 fusion.62
  309.0 10.0 %fusion.60 = (f32[4,512]{1,0:T(4,128)S(1)}, f32[2048,512,4]{1,0,2:T(8,128)}) fusion(pred[512,2048]{0,1:T(8,128)(4,1)S(1)} %broadcast_compare_fusion.2, bf16[512,1,4,128]{3,0,2,1:T(8,128)(2,1)} %get-tuple-element.233, bf16[4,2048,1,128]{3,1,2,0:T(8,128)(2,1)} %get-tuple-element.232, s32[]{:T(128)} %get-tuple-element.215), kind=kOutput, calls=%fused_computation.2.clone.1 | convolution fusion | flops 1086322688 | bytes 18883072 | tf_op jit(solution)/shard_map/while/body/eval_jaxpr/tgcd,sgd->gcts/dot_general | solution.py:68
  319.0 8.7 %fusion.63 = f32[1,4,512,128]{3,2,1,0:T(8,128)S(1)} fusion(f32[2048,512,4]{1,0,2:T(8,128)} %get-tuple-element.202, f32[4,512]{1,0:T(4,128)S(1)} %bitcast.105, pred[512,2048]{0,1:T(8,128)(4,1)S(1)} %broadcast_compare_fusion.2, f32[1,4,512,128]{3,2,1,0:T(8,128)S(1)} %get-tuple-element.218, bf16[4,2048,1,128]{3,1,2,0:T(8,128)(2,1)} %get-tuple-element.234, ...), kind=kOutput, calls=%fused_computation.10.clone.1 | convolution fusion | flops 1095499776 | bytes 20464128 | tf_op jit(solution)/shard_map/while/body/eval_jaxpr/gcts,sgd->gctd/dot_general | solution.py:77
  329.7 4.2 fusion.62
  334.7 10.0 %fusion.60 = (f32[4,512]{1,0:T(4,128)S(1)}, f32[2048,512,4]{1,0,2:T(8,128)}) fusion(pred[512,2048]{0,1:T(8,128)(4,1)S(1)} %broadcast_compare_fusion.2, bf16[512,1,4,128]{3,0,2,1:T(8,128)(2,1)} %get-tuple-element.233, bf16[4,2048,1,128]{3,1,2,0:T(8,128)(2,1)} %get-tuple-element.232, s32[]{:T(128)} %get-tuple-element.215), kind=kOutput, calls=%fused_computation.2.clone.1 | convolution fusion | flops 1086322688 | bytes 18883072 | tf_op jit(solution)/shard_map/while/body/eval_jaxpr/tgcd,sgd->gcts/dot_general | solution.py:68
  344.7 8.7 %fusion.63 = f32[1,4,512,128]{3,2,1,0:T(8,128)S(1)} fusion(f32[2048,512,4]{1,0,2:T(8,128)} %get-tuple-element.202, f32[4,512]{1,0:T(4,128)S(1)} %bitcast.105, pred[512,2048]{0,1:T(8,128)(4,1)S(1)} %broadcast_compare_fusion.2, f32[1,4,512,128]{3,2,1,0:T(8,128)S(1)} %get-tuple-element.218, bf16[4,2048,1,128]{3,1,2,0:T(8,128)(2,1)} %get-tuple-element.234, ...), kind=kOutput, calls=%fused_computation.10.clone.1 | convolution fusion | flops 1095499776 | bytes 20464128 | tf_op jit(solution)/shard_map/while/body/eval_jaxpr/gcts,sgd->gctd/dot_general | solution.py:77
  355.4 4.2 fusion.62
  360.5 10.2 %convolution_convert_fusion = bf16[512,8192]{1,0:T(8,128)(2,1)} fusion(bf16[512,512]{1,0:T(8,128)(2,1)S(1)} %bitcast.111, bf16[512,8192]{1,0:T(8,128)(2,1)} %all-gather.12.cloned.1.call-done), kind=kOutput, calls=%fused_computation.34 | convolution fusion | flops 4299161600 | bytes 17301504 | tf_op jit(solution)/shard_map/dot_general | solution.py:113
  370.8 115.3 %reduce-scatter.2.cloned.1.call-done = bf16[512,1024]{1,0:T(8,128)(2,1)} async-done(((bf16[512,8192]{1,0:T(8,128)(2,1)}), bf16[512,1024]{1,0:T(8,128)(2,1)}) %reduce-scatter.2.cloned.1.call-update) | async-done | bytes 1048592 | tf_op jit(solution)/shard_map/reduce_scatter | solution.py:118
  486.0 2.6 add_convert_fusion
  (74 shorter events, 24.4 us)
Async XLA Ops:
  7.2 185.9 %copy-start.5 = (f32[8192]{0:T(1024)S(1)}, f32[8192]{0:T(1024)}, u32[]{:S(2)}) copy-start(f32[8192]{0:T(1024)} %param.14) | copy-start | bytes 98308
  7.2 114.1 %all-gather.6.cloned.1.call-start = ((), (), s32[]{:S(2)}) async-start(), calls=%async_computation.1 | async-start | bytes 9437184 | tf_op jit(solution)/shard_map/all_gather | solution.py:37
  7.9 185.2 %all-gather.8.cloned.1.call-start = ((), (), s32[]{:S(2)}) async-start(), calls=%async_computation.2 | async-start | bytes 13369344 | tf_op jit(solution)/shard_map/all_gather | solution.py:44
  10.1 235.1 %all-gather.10.cloned.1.call-start = ((), (), s32[]{:S(2)}) async-start(), calls=%async_computation.3 | async-start | bytes 4456448 | tf_op jit(solution)/shard_map/all_gather | solution.py:19
  126.3 82.3 %copy-start.4 = (s32[512]{0:T(512)S(1)}, s32[512]{0:T(512)}, u32[]{:S(2)}) copy-start(s32[512]{0:T(512)} %param.13) | copy-start | bytes 6148
  207.0 153.5 %all-gather.12.cloned.1.call-start = ((), (), s32[]{:S(2)}) async-start(), calls=%async_computation.4 | async-start | bytes 8912896 | tf_op jit(solution)/shard_map/all_gather | solution.py:115
  207.6 278.5 %reduce-scatter.2.cloned.1.call-start = ((), (), s32[]{:S(2)}) async-start(), calls=%async_computation.5 | async-start | bytes 9437184 | tf_op jit(solution)/shard_map/reduce_scatter | solution.py:118
  230.0 25.7 %copy-start.2 = (f32[1,4,512,128]{3,2,1,0:T(8,128)S(1)}, f32[1,4,512,128]{3,2,1,0:T(8,128)}, u32[]{:S(2)}) copy-start(f32[1,4,512,128]{3,2,1,0:T(8,128)} %custom-call.2) | copy-start | bytes 3145732
  266.6 11.3 %copy-start = (f32[2048,512,4]{1,0,2:T(8,128)S(1)}, f32[2048,512,4]{1,0,2:T(8,128)}, u32[]{:S(2)}) copy-start(f32[2048,512,4]{1,0,2:T(8,128)} %get-tuple-element.202) | copy-start | bytes 50331652 | tf_op jit(solution)/shard_map/while
  293.1 10.9 %copy-start = (f32[2048,512,4]{1,0,2:T(8,128)S(1)}, f32[2048,512,4]{1,0,2:T(8,128)}, u32[]{:S(2)}) copy-start(f32[2048,512,4]{1,0,2:T(8,128)} %get-tuple-element.202) | copy-start | bytes 50331652 | tf_op jit(solution)/shard_map/while
  319.0 10.7 %copy-start = (f32[2048,512,4]{1,0,2:T(8,128)S(1)}, f32[2048,512,4]{1,0,2:T(8,128)}, u32[]{:S(2)}) copy-start(f32[2048,512,4]{1,0,2:T(8,128)} %get-tuple-element.202) | copy-start | bytes 50331652 | tf_op jit(solution)/shard_map/while
  344.7 10.7 %copy-start = (f32[2048,512,4]{1,0,2:T(8,128)S(1)}, f32[2048,512,4]{1,0,2:T(8,128)}, u32[]{:S(2)}) copy-start(f32[2048,512,4]{1,0,2:T(8,128)} %get-tuple-element.202) | copy-start | bytes 50331652 | tf_op jit(solution)/shard_map/while
  360.5 10.3 %copy-start.3 = (bf16[64,8,4,128]{3,1,2,0:T(8,128)(2,1)}, bf16[64,8,4,128]{3,1,2,0:T(8,128)(2,1)S(1)}, u32[]{:S(2)}) copy-start(bf16[64,8,4,128]{3,1,2,0:T(8,128)(2,1)S(1)} %copy.39) | copy-start | bytes 1572868
  370.7 115.3 %copy-start.1 = (bf16[512,1024]{1,0:T(8,128)(2,1)S(1)}, bf16[512,1024]{1,0:T(8,128)(2,1)}, u32[]{:S(2)}) copy-start(bf16[512,1024]{1,0:T(8,128)(2,1)} %param.12) | copy-start | bytes 3145732
Sparse Core Ops, SparseCore 0:
  10.3 110.8 all-gather.5
  123.5 69.5 all-gather.7
  207.1 38.0 all-gather.9
  246.8 52.1 all-gather.11
  370.9 115.1 reduce-scatter.1
where the time goes:
time: 496 us; the launch traced here: 495 us
  waiting for transfers between devices  308 us (62%)
  matrix products  98.3 us (20%)
  other arithmetic  35.1 us (7%)
  local copies, waits for them, and re-layouts  20.2 us (4%)
  blocking collectives  19 us (4%)
  between operations  14 us (3%)
    reduce_scatter x1, waiting for transfers between devices, shards(): lax.psum_scatter(out_terms.astype(jnp.bfloat16), 'tensor', scatter_dimens...  115 us
    all_gather x1, waiting for transfers between devices, shards(): features = lax.all_gather(tokens, 'tensor', axis=1, tiled=True)  110 us
    all_gather x1, waiting for transfers between devices, shards(): lax.all_gather(w_cat, 'seq', axis=0, tiled=True)  66.7 us
    dot_general x4, matrix products, attend_block(): jnp.einsum('tgcd,sgd->gcts', queries, block_keys, preferred_element_type=...  40.3 us
    dot_general x4, matrix products, attend_block(): jnp.einsum('gcts,sgd->gctd', weights.astype(jnp.bfloat16), block_values,...  35.2 us
    all_gather x1, blocking collectives, shards(): lax.all_gather(positions, 'seq', axis=0, tiled=True)  19 us
    reduce_sum x4, other arithmetic, attend_block(): denominator = denominator * rescale + jnp.sum(weights, -1)  16.6 us
    all_gather x1, waiting for transfers between devices, sent_together(): lax.all_gather(both, axis, axis=dim, tiled=True)  15.2 us
  transfers between devices with their start and end apart: 5, of which 4 were waited for; matrix products, arithmetic and copies ran while one was open for 24% of the time, Pallas kernels for 0%

commit v1 on v0

--- a/solution.py
+++ b/solution.py
@@ -34,7 +34,9 @@
 
 def shards(tokens, positions, norm_gain, w_query, w_key, w_value, b_query, b_key, b_value, w_out):
     tok_rows = tokens.shape[0]
-    features = lax.all_gather(tokens, "tensor", axis=1, tiled=True)
+    features = jnp.concatenate(
+        lax.all_to_all(jnp.stack([tokens] * lax.axis_size("tensor")), "tensor", 0, 0), axis=1
+    )
     inputs = features.astype(jnp.float32)
     inverse_rms = lax.rsqrt(jnp.mean(inputs * inputs, -1, keepdims=True) + NORM_EPS)
     normed = (inputs * inverse_rms * norm_gain[None, :]).astype(jnp.bfloat16)

time: 496 us -> 476 us (0.960)
  waiting for transfers between devices: 308 us -> 269 us
  starting transfers between devices: 0.2 us -> 8.03 us
  other arithmetic: 35.1 us -> 41.8 us
  local copies, waits for them, and re-layouts: 20.2 us -> 25.7 us
    all_to_all x0 -> x1, waiting for transfers between devices: none -> 117 us  [shards(): lax.all_to_all(jnp.stack([tokens] * lax.axis_size('tensor')), 'tensor', 0...]
    all_gather x1 -> x0, waiting for transfers between devices: 110 us -> none  [shards(): features = lax.all_gather(tokens, 'tensor', axis=1, tiled=True)]
    all_gather x1, waiting for transfers between devices: 66.7 us -> 21.3 us  [shards(): lax.all_gather(w_cat, 'seq', axis=0, tiled=True)]
    convert_element_type x0 -> x1, other arithmetic: none -> 7.88 us  [shards(): normed = (inputs * inverse_rms * norm_gain[None, :]).astype(jnp.bfloat16)]
    all_to_all x0 -> x1, starting transfers between devices: none -> 7.87 us  [shards(): lax.all_to_all(jnp.stack([tokens] * lax.axis_size('tensor')), 'tensor', 0...]
  transfers between devices with their start and end apart: 5 -> 5, of which waited for: 4 -> 4; matrix products, arithmetic and copies ran while one was open for 24% -> 27% of each run, Pallas kernels for 0% -> 0%
where the time goes in v1:
time: 476 us; the launch traced here: 475 us
  waiting for transfers between devices  269 us (57%)
  matrix products  97.8 us (21%)
  other arithmetic  41.8 us (9%)
  local copies, waits for them, and re-layouts  25.7 us (5%)
  blocking collectives  18.8 us (4%)
  between operations  14 us (3%)
  starting transfers between devices  8.03 us (2%)
    all_to_all x1, waiting for transfers between devices, shards(): lax.all_to_all(jnp.stack([tokens] * lax.axis_size('tensor')), 'tensor', 0...  117 us
    reduce_scatter x1, waiting for transfers between devices, shards(): lax.psum_scatter(out_terms.astype(jnp.bfloat16), 'tensor', scatter_dimens...  115 us
    dot_general x4, matrix products, attend_block(): jnp.einsum('tgcd,sgd->gcts', queries, block_keys, preferred_element_type=...  40.3 us
    dot_general x4, matrix products, attend_block(): jnp.einsum('gcts,sgd->gctd', weights.astype(jnp.bfloat16), block_values,...  35.2 us
    all_gather x1, waiting for transfers between devices, shards(): lax.all_gather(w_cat, 'seq', axis=0, tiled=True)  21.3 us
    all_gather x1, blocking collectives, shards(): lax.all_gather(positions, 'seq', axis=0, tiled=True)  18.8 us
    reduce_sum x4, other arithmetic, attend_block(): denominator = denominator * rescale + jnp.sum(weights, -1)  16.6 us
    all_gather x1, waiting for transfers between devices, sent_together(): lax.all_gather(both, axis, axis=dim, tiled=True)  15 us
  transfers between devices with their start and end apart: 5, of which 4 were waited for; matrix products, arithmetic and copies ran while one was open for 27% of the time, Pallas kernels for 0%

profile of v1, /device:TPU:0, one launch (start us, length us, event | category | flops | bytes accessed | tf_op | source)
XLA Modules:
  0.0 475.3 jit_solution(18070897689401060275)
XLA Ops:
  14.9 7.9 %all-to-all-start = ((bf16[8,512,1024]{1,2,0:T(8,128)(2,1)}), bf16[8,512,1024]{1,2,0:T(8,128)(2,1)}, u32[]{:S(2)}, u32[]{:S(2)}) async-start(bf16[8,512,1024]{1,2,0:T(8,128)(2,1)} %stack.2), calls=%async_computation | async-start | bytes 16777216 | tf_op jit(solution)/shard_map/all_to_all | solution.py:38
  22.9 117.1 %all-to-all-done = bf16[8,512,1024]{1,2,0:T(8,128)(2,1)} async-done(((bf16[8,512,1024]{1,2,0:T(8,128)(2,1)}), bf16[8,512,1024]{1,2,0:T(8,128)(2,1)}, u32[]{:S(2)}, u32[]{:S(2)}) %all-to-all-start) | async-done | bytes 8388640 | tf_op jit(solution)/shard_map/all_to_all | solution.py:38
  140.0 5.3 %multiply_reduce_fusion = f32[512]{0:T(512)S(1)} fusion(bf16[8,512,1024]{1,2,0:T(8,128)(2,1)} %all-to-all-done), kind=kLoop, calls=%fused_computation.32 | loop fusion | flops 12582400 | bytes 8390656 | tf_op jit(solution)/shard_map/reduce_sum | solution.py:41
  145.3 7.9 %fusion.26 = bf16[512,8192]{0,1:T(8,128)(2,1)} fusion(f32[8192]{0:T(1024)S(1)} %copy-done.5, f32[512]{0:T(512)S(1)} %add_rsqrt_fusion, bf16[8,512,1024]{1,2,0:T(8,128)(2,1)} %all-to-all-done), kind=kLoop, calls=%fused_computation.31 | loop fusion | flops 16777216 | bytes 16812032 | tf_op jit(solution)/shard_map/convert_element_type | solution.py:42
  153.2 21.3 %all-gather.5.cloned.1.call-done = bf16[8192,768]{1,0:T(8,128)(2,1)} async-done(((bf16[512,768]{1,0:T(8,128)(2,1)}), bf16[8192,768]{1,0:T(8,128)(2,1)}) %all-gather.5.cloned.1.call-update) | async-done | bytes 12582928 | tf_op jit(solution)/shard_map/all_gather | solution.py:46
  174.5 12.0 %convolution_add_fusion = f32[512,768]{0,1:T(8,128)S(1)} fusion(bf16[512,8192]{0,1:T(8,128)(2,1)} %fusion.26, bf16[8192,768]{1,0:T(8,128)(2,1)} %all-gather.5.cloned.1.call-done, f32[768]{0:T(1024)S(1)} %pad_maximum_fusion.3), kind=kOutput, calls=%fused_computation.35 | convolution fusion | flops 6442844160 | bytes 22547456 | tf_op jit(solution)/shard_map/dot_general | solution.py:45
  189.7 18.8 %all-gather = s32[16,1,512]{2,1,0:T(1,128)S(1)} all-gather(s32[1,1,512]{2,1,0:T(1,128)S(1)} %bitcast.123), channel_id=1, replica_groups=mesh['seq'=16,'tensor'=8] {'seq'}, dimensions={0}, use_global_device_ids=true | all-gather | bytes 34816 | tf_op jit(solution)/shard_map/all_gather | solution.py:94
  210.9 15.0 %all-gather.7.cloned.1.call-done = bf16[8192,2,128]{0,2,1:T(8,128)(2,1)} async-done(((bf16[512,2,128]{0,2,1:T(8,128)(2,1)}), bf16[8192,2,128]{0,2,1:T(8,128)(2,1)}) %all-gather.7.cloned.1.call-update) | async-done | bytes 4194320 | tf_op jit(solution)/shard_map/all_gather | solution.py:19
  229.8 4.1 copy.42
  236.4 103.9 %while.15 = (s32[]{:T(128)}, f32[1,4,512]{2,1,0:T(4,128)S(1)}, f32[1,4,512]{2,1,0:T(4,128)S(1)}, f32[1,4,512,128]{3,2,1,0:T(8,128)S(1)}, s32[4,2048]{1,0:T(4,128...) while((s32[]{:T(128)}, f32[1,4,512]{2,1,0:T(4,128)S(1)}, ...), condition=%wide.region_4.5_spmd.clone, body=%wide.region_1.4_spmd.clone.sunk | while | flops 2203856896 | bytes 125463704 | solution.py:107
  237.1 10.2 %fusion.53 = (f32[4,512]{1,0:T(4,128)S(1)}, f32[2048,512,4]{1,0,2:T(8,128)}) fusion(pred[512,2048]{0,1:T(8,128)(4,1)S(1)} %broadcast_compare_fusion.2, bf16[512,1,4,128]{3,0,2,1:T(8,128)(2,1)} %get-tuple-element.242, bf16[4,2048,1,128]{3,1,2,0:T(8,128)(2,1)} %get-tuple-element.241, s32[]{:T(128)} %get-tuple-element.224), kind=kOutput, calls=%fused_computation.2.clone.1 | convolution fusion | flops 1086322688 | bytes 18883072 | tf_op jit(solution)/shard_map/while/body/eval_jaxpr/tgcd,sgd->gcts/dot_general | solution.py:70
  247.3 9.0 %fusion.56 = f32[1,4,512,128]{3,2,1,0:T(8,128)S(1)} fusion(f32[2048,512,4]{1,0,2:T(8,128)} %get-tuple-element.211, f32[4,512]{1,0:T(4,128)S(1)} %bitcast.114, pred[512,2048]{0,1:T(8,128)(4,1)S(1)} %broadcast_compare_fusion.2, f32[1,4,512,128]{3,2,1,0:T(8,128)S(1)} %get-tuple-element.227, bf16[4,2048,1,128]{3,1,2,0:T(8,128)(2,1)} %get-tuple-element.243, ...), kind=kOutput, calls=%fused_computation.10.clone.1 | convolution fusion | flops 1095499776 | bytes 20464128 | tf_op jit(solution)/shard_map/while/body/eval_jaxpr/gcts,sgd->gctd/dot_general | solution.py:79
  258.6 4.2 fusion.55
  263.6 10.2 %fusion.53 = (f32[4,512]{1,0:T(4,128)S(1)}, f32[2048,512,4]{1,0,2:T(8,128)}) fusion(pred[512,2048]{0,1:T(8,128)(4,1)S(1)} %broadcast_compare_fusion.2, bf16[512,1,4,128]{3,0,2,1:T(8,128)(2,1)} %get-tuple-element.242, bf16[4,2048,1,128]{3,1,2,0:T(8,128)(2,1)} %get-tuple-element.241, s32[]{:T(128)} %get-tuple-element.224), kind=kOutput, calls=%fused_computation.2.clone.1 | convolution fusion | flops 1086322688 | bytes 18883072 | tf_op jit(solution)/shard_map/while/body/eval_jaxpr/tgcd,sgd->gcts/dot_general | solution.py:70
  273.8 8.8 %fusion.56 = f32[1,4,512,128]{3,2,1,0:T(8,128)S(1)} fusion(f32[2048,512,4]{1,0,2:T(8,128)} %get-tuple-element.211, f32[4,512]{1,0:T(4,128)S(1)} %bitcast.114, pred[512,2048]{0,1:T(8,128)(4,1)S(1)} %broadcast_compare_fusion.2, f32[1,4,512,128]{3,2,1,0:T(8,128)S(1)} %get-tuple-element.227, bf16[4,2048,1,128]{3,1,2,0:T(8,128)(2,1)} %get-tuple-element.243, ...), kind=kOutput, calls=%fused_computation.10.clone.1 | convolution fusion | flops 1095499776 | bytes 20464128 | tf_op jit(solution)/shard_map/while/body/eval_jaxpr/gcts,sgd->gctd/dot_general | solution.py:79
  284.7 4.2 fusion.55
  289.7 10.0 %fusion.53 = (f32[4,512]{1,0:T(4,128)S(1)}, f32[2048,512,4]{1,0,2:T(8,128)}) fusion(pred[512,2048]{0,1:T(8,128)(4,1)S(1)} %broadcast_compare_fusion.2, bf16[512,1,4,128]{3,0,2,1:T(8,128)(2,1)} %get-tuple-element.242, bf16[4,2048,1,128]{3,1,2,0:T(8,128)(2,1)} %get-tuple-element.241, s32[]{:T(128)} %get-tuple-element.224), kind=kOutput, calls=%fused_computation.2.clone.1 | convolution fusion | flops 1086322688 | bytes 18883072 | tf_op jit(solution)/shard_map/while/body/eval_jaxpr/tgcd,sgd->gcts/dot_general | solution.py:70
  299.7 8.7 %fusion.56 = f32[1,4,512,128]{3,2,1,0:T(8,128)S(1)} fusion(f32[2048,512,4]{1,0,2:T(8,128)} %get-tuple-element.211, f32[4,512]{1,0:T(4,128)S(1)} %bitcast.114, pred[512,2048]{0,1:T(8,128)(4,1)S(1)} %broadcast_compare_fusion.2, f32[1,4,512,128]{3,2,1,0:T(8,128)S(1)} %get-tuple-element.227, bf16[4,2048,1,128]{3,1,2,0:T(8,128)(2,1)} %get-tuple-element.243, ...), kind=kOutput, calls=%fused_computation.10.clone.1 | convolution fusion | flops 1095499776 | bytes 20464128 | tf_op jit(solution)/shard_map/while/body/eval_jaxpr/gcts,sgd->gctd/dot_general | solution.py:79
  310.4 4.2 fusion.55
  315.4 10.0 %fusion.53 = (f32[4,512]{1,0:T(4,128)S(1)}, f32[2048,512,4]{1,0,2:T(8,128)}) fusion(pred[512,2048]{0,1:T(8,128)(4,1)S(1)} %broadcast_compare_fusion.2, bf16[512,1,4,128]{3,0,2,1:T(8,128)(2,1)} %get-tuple-element.242, bf16[4,2048,1,128]{3,1,2,0:T(8,128)(2,1)} %get-tuple-element.241, s32[]{:T(128)} %get-tuple-element.224), kind=kOutput, calls=%fused_computation.2.clone.1 | convolution fusion | flops 1086322688 | bytes 18883072 | tf_op jit(solution)/shard_map/while/body/eval_jaxpr/tgcd,sgd->gcts/dot_general | solution.py:70
  325.4 8.7 %fusion.56 = f32[1,4,512,128]{3,2,1,0:T(8,128)S(1)} fusion(f32[2048,512,4]{1,0,2:T(8,128)} %get-tuple-element.211, f32[4,512]{1,0:T(4,128)S(1)} %bitcast.114, pred[512,2048]{0,1:T(8,128)(4,1)S(1)} %broadcast_compare_fusion.2, f32[1,4,512,128]{3,2,1,0:T(8,128)S(1)} %get-tuple-element.227, bf16[4,2048,1,128]{3,1,2,0:T(8,128)(2,1)} %get-tuple-element.243, ...), kind=kOutput, calls=%fused_computation.10.clone.1 | convolution fusion | flops 1095499776 | bytes 20464128 | tf_op jit(solution)/shard_map/while/body/eval_jaxpr/gcts,sgd->gctd/dot_general | solution.py:79
  336.1 4.2 fusion.55
  341.2 10.2 %convolution_convert_fusion = bf16[512,8192]{1,0:T(8,128)(2,1)} fusion(bf16[512,512]{1,0:T(8,128)(2,1)S(1)} %bitcast.120, bf16[512,8192]{1,0:T(8,128)(2,1)} %all-gather.9.cloned.1.call-done), kind=kOutput, calls=%fused_computation.33 | convolution fusion | flops 4299161600 | bytes 17301504 | tf_op jit(solution)/shard_map/dot_general | solution.py:115
  351.5 114.7 %reduce-scatter.2.cloned.1.call-done = bf16[512,1024]{1,0:T(8,128)(2,1)} async-done(((bf16[512,8192]{1,0:T(8,128)(2,1)}), bf16[512,1024]{1,0:T(8,128)(2,1)}) %reduce-scatter.2.cloned.1.call-update) | async-done | bytes 1048592 | tf_op jit(solution)/shard_map/reduce_scatter | solution.py:120
  (82 shorter events, 34.5 us)
Async XLA Ops:
  7.2 167.3 %all-gather.5.cloned.1.call-start = ((), (), s32[]{:S(2)}) async-start(), calls=%async_computation.2 | async-start | bytes 13369344 | tf_op jit(solution)/shard_map/all_gather | solution.py:46
  14.9 7.9 %copy-start.4 = (s32[512]{0:T(512)S(1)}, s32[512]{0:T(512)}, u32[]{:S(2)}) copy-start(s32[512]{0:T(512)} %param.13) | copy-start | bytes 6148
  14.9 8.0 %copy-start.6 = (f32[512]{0:T(512)S(1)}, f32[512]{0:T(512)}, u32[]{:S(2)}) copy-start(f32[512]{0:T(512)} %param.18) | copy-start | bytes 6148
  14.9 8.0 %copy-start.7 = (f32[128]{0:T(128)S(1)}, f32[128]{0:T(128)}, u32[]{:S(2)}) copy-start(f32[128]{0:T(128)} %param.20) | copy-start | bytes 1540
  14.9 8.0 %copy-start.8 = (f32[128]{0:T(128)S(1)}, f32[128]{0:T(128)}, u32[]{:S(2)}) copy-start(f32[128]{0:T(128)} %param.19) | copy-start | bytes 1540
  14.9 125.1 %all-to-all-start = ((bf16[8,512,1024]{1,2,0:T(8,128)(2,1)}), bf16[8,512,1024]{1,2,0:T(8,128)(2,1)}, u32[]{:S(2)}, u32[]{:S(2)}) async-start(bf16[8,512,1024]{1,2,0:T(8,128)(2,1)} %stack.2), calls=%async_computation | async-start | bytes 16777216 | tf_op jit(solution)/shard_map/all_to_all | solution.py:38
  22.7 122.6 %copy-start.5 = (f32[8192]{0:T(1024)S(1)}, f32[8192]{0:T(1024)}, u32[]{:S(2)}) copy-start(f32[8192]{0:T(1024)} %param.14) | copy-start | bytes 98308
  22.7 203.2 %all-gather.7.cloned.1.call-start = ((), (), s32[]{:S(2)}) async-start(), calls=%async_computation.3 | async-start | bytes 4456448 | tf_op jit(solution)/shard_map/all_gather | solution.py:19
  187.9 153.3 %all-gather.9.cloned.1.call-start = ((), (), s32[]{:S(2)}) async-start(), calls=%async_computation.4 | async-start | bytes 8912896 | tf_op jit(solution)/shard_map/all_gather | solution.py:117
  188.6 277.6 %reduce-scatter.2.cloned.1.call-start = ((), (), s32[]{:S(2)}) async-start(), calls=%async_computation.5 | async-start | bytes 9437184 | tf_op jit(solution)/shard_map/reduce_scatter | solution.py:120
  210.9 25.5 %copy-start.2 = (f32[1,4,512,128]{3,2,1,0:T(8,128)S(1)}, f32[1,4,512,128]{3,2,1,0:T(8,128)}, u32[]{:S(2)}) copy-start(f32[1,4,512,128]{3,2,1,0:T(8,128)} %custom-call.2) | copy-start | bytes 3145732
  247.3 11.3 %copy-start = (f32[2048,512,4]{1,0,2:T(8,128)S(1)}, f32[2048,512,4]{1,0,2:T(8,128)}, u32[]{:S(2)}) copy-start(f32[2048,512,4]{1,0,2:T(8,128)} %get-tuple-element.211) | copy-start | bytes 50331652 | tf_op jit(solution)/shard_map/while
  273.8 10.9 %copy-start = (f32[2048,512,4]{1,0,2:T(8,128)S(1)}, f32[2048,512,4]{1,0,2:T(8,128)}, u32[]{:S(2)}) copy-start(f32[2048,512,4]{1,0,2:T(8,128)} %get-tuple-element.211) | copy-start | bytes 50331652 | tf_op jit(solution)/shard_map/while
  299.7 10.7 %copy-start = (f32[2048,512,4]{1,0,2:T(8,128)S(1)}, f32[2048,512,4]{1,0,2:T(8,128)}, u32[]{:S(2)}) copy-start(f32[2048,512,4]{1,0,2:T(8,128)} %get-tuple-element.211) | copy-start | bytes 50331652 | tf_op jit(solution)/shard_map/while
  325.4 10.7 %copy-start = (f32[2048,512,4]{1,0,2:T(8,128)S(1)}, f32[2048,512,4]{1,0,2:T(8,128)}, u32[]{:S(2)}) copy-start(f32[2048,512,4]{1,0,2:T(8,128)} %get-tuple-element.211) | copy-start | bytes 50331652 | tf_op jit(solution)/shard_map/while
  341.2 10.3 %copy-start.3 = (bf16[64,8,4,128]{3,1,2,0:T(8,128)(2,1)}, bf16[64,8,4,128]{3,1,2,0:T(8,128)(2,1)S(1)}, u32[]{:S(2)}) copy-start(bf16[64,8,4,128]{3,1,2,0:T(8,128)(2,1)S(1)} %copy.48) | copy-start | bytes 1572868
  351.4 114.8 %copy-start.1 = (bf16[512,1024]{1,0:T(8,128)(2,1)S(1)}, bf16[512,1024]{1,0:T(8,128)(2,1)}, u32[]{:S(2)}) copy-start(bf16[512,1024]{1,0:T(8,128)(2,1)} %param.12) | copy-start | bytes 3145732
Sparse Core Ops, SparseCore 0:
  10.2 164.2 all-gather.4
  188.0 37.8 all-gather.6
  227.6 52.1 all-gather.8
  351.6 114.5 reduce-scatter.1
